TPU v7x, 32 devices: a whole 2x2x4 slice. The times are simulated.
32 devices in a mesh: comp: 2 (over core), tgt: 4 (over y, x), src: 4 (over z).
Axes of the slice: x: 2, y: 2, z: 4, core: 2. Of those that a mesh axis runs over, the one named last changes fastest.
Arguments:
- field: bfloat16 [3, 32, 8192], P(None, None, ('tgt', 'src')), may hold values from -6 to 6
- dest_group: int32 [4096, 1], P(('comp', 'tgt', 'src')), may hold values from 0 to 3; in each aligned block of 128 rows (0 to 127, 128 to 255, ...) at most 64 rows name the same one
- src_local: int32 [4096], P(('comp', 'tgt', 'src')), may hold values from 0 to 1
- ranks: int32 [4096], P(('comp', 'tgt', 'src')), may hold values from 8 to 64
- mixing: float32 [4096, 3, 3], P(('comp', 'tgt', 'src')), may hold values from -5 to 5
- v_factor: bfloat16 [4096, 64, 256], P(('comp', 'tgt', 'src')), may hold values from -0.375 to 0.375
- u_factor: bfloat16 [8192, 64, 256], P(('comp', 'tgt', 'src')), may hold values from -0.0625 to 0.0625
- slot_cluster: int32 [8192], P(('comp', 'tgt', 'src')), may hold values from 0 to 7
- near_src: int32 [128], P(('comp', 'tgt', 'src')), may hold values from 0 to 1
- near_tgt: int32 [128], P(('comp', 'tgt', 'src')), may hold values from 0 to 7
- near_mixing: float32 [128, 3, 3], P(('comp', 'tgt', 'src')), may hold values from -5 to 5
- near_matrix: bfloat16 [128, 256, 256], P(('comp', 'tgt', 'src')), may hold values from -0.1875 to 0.1875
Outputs:
- result: float32 [3, 32, 8192], P(None, None, ('comp', 'tgt', 'src'))
Inputs may be any that keep to these rules, and one draw needn't show every extreme that they name: `dest_group`: among the 128 blocks of one device at most 64 name the same target group, and in every draw some device has exactly 64 blocks to one group.
All inputs are finite; a program needn't handle non-finite values.
Results may differ from a plain program's by a relative error of at most 0.0018.
Values may be sent and summed in bfloat16 or wider, within the bound.
A program may use at most 128 MiB of HBM per device.

v0:
```python
import jax
import jax.numpy as jnp
from jax import lax
from jax.sharding import PartitionSpec as P


def body(
    field,
    dest_group,
    src_local,
    ranks,
    mixing,
    v_factor,
    u_factor,
    slot_cluster,
    near_src,
    near_tgt,
    near_mixing,
    near_matrix,
):
    groups = lax.axis_size("tgt")
    shards = lax.axis_size("src")
    pairing = lax.axis_size("comp")
    blocks, rank_width, cluster_size = v_factor.shape
    components, vectors, points = field.shape
    channels = components * vectors
    owned_clusters = points // cluster_size
    slot_count = u_factor.shape[0]
    capacity = slot_count // groups
    targets = owned_clusters * shards
    near_count = near_matrix.shape[0]
    sources = field.reshape(channels, owned_clusters, cluster_size)
    highest = lax.Precision.HIGHEST
    chosen = (src_local[:, None] == jnp.arange(owned_clusters, dtype=jnp.int32)[None, :]).astype(
        jnp.bfloat16
    )
    selected = jnp.einsum(
        "bk,fkp->bfp", chosen, sources, preferred_element_type=jnp.float32
    ).astype(jnp.bfloat16)
    coefficients = jnp.einsum(
        "bfp,brp->bfr", selected, v_factor, preferred_element_type=jnp.float32
    )
    rank_mask = (jnp.arange(rank_width, dtype=jnp.int32)[None, :] < ranks[:, None]).astype(
        jnp.float32
    )
    coefficients = (coefficients * rank_mask[:, None, :]).reshape(
        blocks, components, vectors, rank_width
    )
    mixed_coef = jnp.einsum("bcd,bdsr->bcsr", mixing, coefficients, precision=highest)
    mixed_coef = mixed_coef.reshape(blocks, channels * rank_width).astype(jnp.bfloat16)
    destination = dest_group[:, 0]
    member = (destination[:, None] == jnp.arange(groups, dtype=jnp.int32)[None, :]).astype(
        jnp.int32
    )
    position = jnp.sum(jnp.cumsum(member, axis=0) * member, axis=1) - 1
    slot_of = destination * capacity + position
    placing = (slot_of[:, None] == jnp.arange(slot_count, dtype=jnp.int32)[None, :]).astype(
        jnp.bfloat16
    )
    outgoing = jnp.einsum(
        "bs,bf->sf", placing, mixed_coef, preferred_element_type=jnp.float32
    ).astype(jnp.bfloat16)
    outgoing = outgoing.reshape(groups, capacity, channels * rank_width)
    incoming = lax.all_to_all(outgoing, "tgt", split_axis=0, concat_axis=0, tiled=True)
    near_chosen = (
        near_src[:, None] == jnp.arange(owned_clusters, dtype=jnp.int32)[None, :]
    ).astype(jnp.bfloat16)
    near_inputs = jnp.einsum(
        "nk,fkp->nfp", near_chosen, sources, preferred_element_type=jnp.float32
    ).astype(jnp.bfloat16)
    dense_out = jnp.einsum(
        "nfp,nqp->nfq", near_inputs, near_matrix, preferred_element_type=jnp.float32
    )
    dense_out = dense_out.reshape(near_count, components, vectors, cluster_size)
    mixed_near = jnp.einsum("ncd,ndsq->ncsq", near_mixing, dense_out, precision=highest).reshape(
        near_count, channels, cluster_size
    )
    near_spread = (near_tgt[:, None] == jnp.arange(targets, dtype=jnp.int32)[None, :]).astype(
        jnp.float32
    )
    near_part = jnp.einsum("nt,nfq->ftq", near_spread, mixed_near, precision=highest)
    received = incoming.reshape(slot_count, channels, rank_width)
    contrib = jnp.einsum("sfr,srq->sfq", received, u_factor, preferred_element_type=jnp.float32)
    far_spread = (slot_cluster[:, None] == jnp.arange(targets, dtype=jnp.int32)[None, :]).astype(
        jnp.float32
    )
    far_part = jnp.einsum("st,sfq->ftq", far_spread, contrib, precision=highest)
    partial_value = far_part + near_part
    half_owned = targets // (pairing * shards)
    sectioned = partial_value.reshape(channels, pairing, shards, half_owned, cluster_size)
    sectioned = lax.psum_scatter(sectioned, "src", scatter_dimension=2, tiled=True)
    summed = lax.psum_scatter(sectioned, "comp", scatter_dimension=1, tiled=True)
    return summed.reshape(components, vectors, half_owned * cluster_size)


def solution(mesh):
    placed = (
        P(None, None, ("tgt", "src")),
        P(("comp", "tgt", "src"), None),
        P(("comp", "tgt", "src")),
        P(("comp", "tgt", "src")),
        P(("comp", "tgt", "src"), None, None),
        P(("comp", "tgt", "src"), None, None),
        P(("comp", "tgt", "src"), None, None),
        P(("comp", "tgt", "src")),
        P(("comp", "tgt", "src")),
        P(("comp", "tgt", "src")),
        P(("comp", "tgt", "src"), None, None),
        P(("comp", "tgt", "src"), None, None),
    )
    return jax.shard_map(
        body,
        mesh=mesh,
        in_specs=placed,
        out_specs=P(None, None, ("comp", "tgt", "src")),
        check_vma=False,
    )
```

profile of v0, /device:TPU:0, one launch (start us, length us, event | category | flops | bytes accessed | tf_op | source)
XLA Modules:
  0.0 195.1 jit_solution(940742748221658670)
XLA Ops:
  6.5 0.0 copy-start
  6.5 0.8 fusion.15
  7.3 0.2 reduce_window_sum.11
  7.5 0.8 select_reduce_fusion
  8.3 0.7 fusion.30
  9.0 0.9 reshape.57
  9.9 0.0 copy-start.2
  9.9 0.9 fusion.16
  10.8 2.7 %convolution_convert_fusion.2 = bf16[128,96,256]{2,0,1:T(8,128)(2,1)S(1)} fusion(bf16[96,2,256]{2,1,0:T(2,128)(2,1)S(1)} %reshape.57, s32[128]{0:T(128)} %param.14), kind=kOutput, calls=%fused_computation.7 | convolution fusion | flops 15728896 | bytes 6390272 | tf_op jit(solution)/shard_map/bk,fkp->bfp/dot_general | solution.py:37
  13.6 0.0 copy-done.2
  13.6 9.1 %broadcast_multiply_fusion = f32[128,96,64]{1,2,0:T(8,128)} fusion(f32[128,64]{1,0:T(8,128)S(1)} %fusion.16, bf16[128,64,256]{2,1,0:T(8,128)(2,1)S(1)} %copy-done.2, bf16[128,96,256]{2,0,1:T(8,128)(2,1)S(1)} %convolution_convert_fusion.2), kind=kOutput, calls=%fused_computation.8 | convolution fusion | flops 403439616 | bytes 13664256 | tf_op jit(solution)/shard_map/bfp,brp->bfr/dot_general | solution.py:40
  22.6 5.4 %copy.26 = f32[128,96,64]{0,2,1:T(8,128)} copy(f32[128,96,64]{1,2,0:T(8,128)} %broadcast_multiply_fusion) | data formatting | bytes 6291456 | tf_op jit(solution)/shard_map/mul | solution.py:46
  28.0 0.0 copy-start.4
  28.0 7.7 %copy.27 = f32[128,3,32,64]{3,1,2,0:T(4,128)} copy(f32[128,3,32,64]{0,3,2,1:T(8,128)} %bitcast.44) | data formatting | bytes 6291456 | tf_op jit(solution)/shard_map/reshape | solution.py:46
  35.7 0.0 copy-done.4
  35.7 0.2 copy.39
  35.9 18.0 %fusion.4 = bf16[128,3,32,64]{3,1,2,0:T(4,128)(2,1)} fusion(f32[128,3,32,64]{3,1,2,0:T(4,128)} %copy.27, f32[128,3,3,1]{2,1,3,0:T(4,128)S(1)} %copy.39), kind=kOutput, calls=%fused_computation.6 | convolution fusion | flops 29097984 | bytes 4723200 | tf_op jit(solution)/shard_map/bcd,bdsr->bcsr/dot_general | solution.py:49
  53.9 5.9 %copy.29 = bf16[128,3,32,64]{0,3,2,1:T(8,128)(2,1)S(1)} copy(bf16[128,3,32,64]{3,1,2,0:T(4,128)(2,1)} %fusion.4) | data formatting | bytes 3145728 | tf_op jit(solution)/shard_map/convert_element_type | solution.py:50
  59.9 0.0 copy-start.7
  59.9 0.0 copy-start.3
  59.9 2.8 %convolution_convert_fusion = bf16[256,6144]{1,0:T(8,128)(2,1)} fusion(bf16[128,6144]{0,1:T(8,128)(2,1)S(1)} %bitcast.45, s32[128]{0:T(128)S(1)} %fusion.30), kind=kOutput, calls=%fused_computation.2 | convolution fusion | flops 404291584 | bytes 4719104 | tf_op jit(solution)/shard_map/bs,bf->sf/dot_general | solution.py:60
  62.7 5.2 %all-to-all-start = ((bf16[4,64,6144]{2,1,0:T(8,128)(2,1)}), bf16[4,64,6144]{2,1,0:T(8,128)(2,1)}, u32[]{:S(2)}, u32[]{:S(2)}) async-start(bf16[4,64,6144]{2,1,0:T(8,128)(2,1)} %bitcast.43), calls=%async_computation | async-start | bytes 6291456 | tf_op jit(solution)/shard_map/all_to_all | solution.py:64
  67.9 0.0 reduce-scatter.3.cloned.1.call-start
  67.9 0.0 copy-done.7
  67.9 0.3 convolution_convert_fusion.3
  68.2 0.0 copy-done
  68.2 0.3 fusion.10
  68.5 0.0 copy-done.3
  68.5 1.2 convolution_bitcast_fusion
  69.7 0.1 copy.35
  69.8 35.4 %all-to-all-done = bf16[4,64,6144]{2,1,0:T(8,128)(2,1)} async-done(((bf16[4,64,6144]{2,1,0:T(8,128)(2,1)}), bf16[4,64,6144]{2,1,0:T(8,128)(2,1)}, u32[]{:S(2)}, u32[]{:S(2)}) %all-to-all-start) | async-done | bytes 3145760 | tf_op jit(solution)/shard_map/all_to_all | solution.py:64
  105.2 9.6 %reshape.60 = bf16[256,96,64]{2,1,0:T(8,128)(2,1)} reshape(bf16[4,64,6144]{2,1,0:T(8,128)(2,1)} %all-to-all-done) | data formatting | bytes 6291456 | tf_op jit(solution)/shard_map/reshape | solution.py:82
  114.8 0.0 copy-start.5
  114.8 16.9 %fusion.33 = f32[256,96,256]{2,1,0:T(8,128)} fusion(bf16[256,96,64]{2,1,0:T(8,128)(2,1)} %reshape.60, bf16[256,64,256]{2,1,0:T(8,128)(2,1)} %param.18), kind=kOutput, calls=%fused_computation.42 | convolution fusion | flops 805306368 | bytes 36700160 | tf_op jit(solution)/shard_map/sfr,srq->sfq/dot_general | solution.py:83
  131.7 0.0 copy-done.5
  131.7 0.0 copy-start.6
  131.7 0.0 copy-start.1
  131.7 21.2 %fusion = f32[96,256,8]{1,2,0:T(8,128)S(1)} fusion(f32[256,96,256]{2,1,0:T(8,128)} %fusion.33, s32[256]{0:T(256)S(1)} %copy-done.5), kind=kOutput, calls=%fused_computation | convolution fusion | flops 603981824 | bytes 25953280 | tf_op jit(solution)/shard_map/st,sfq->ftq/dot_general | solution.py:87
  152.9 0.0 copy-done.6
  152.9 0.8 fusion.7
  153.7 0.2 reshape.63
  153.9 1.1 copy.37
  155.1 0.0 reduce-scatter.3.cloned.1.call-update
  155.1 0.0 reduce-scatter.5.cloned.1.call-start
  155.1 23.8 %reduce-scatter.3.cloned.1.call-done = f32[96,2,1,1,256]{4,0,3,1,2:T(8,128)} async-done(((f32[96,2,4,1,256]{4,0,3,1,2:T(8,128)}), f32[96,2,1,1,256]{4,0,3,1,2:T(8,128)}) %reduce-scatter.3.cloned.1.call-update) | async-done | bytes 196624 | tf_op jit(solution)/shard_map/reduce_scatter | solution.py:91
  178.9 0.0 reduce-scatter.5.cloned.1.call-update
  178.9 9.4 %reduce-scatter.5.cloned.1.call-done = f32[96,1,1,1,256]{4,0,3,2,1:T(8,128)} async-done(((f32[96,2,1,1,256]{4,0,3,2,1:T(8,128)}), f32[96,1,1,1,256]{4,0,3,2,1:T(8,128)}) %reduce-scatter.5.cloned.1.call-update) | async-done | bytes 98320 | tf_op jit(solution)/shard_map/reduce_scatter | solution.py:92
  188.3 0.0 copy-done.1
Async XLA Ops:
  6.5 61.6 %copy-start = (bf16[4,256,256]{2,1,0:T(8,128)(2,1)S(1)}, bf16[4,256,256]{2,1,0:T(8,128)(2,1)}, u32[]{:S(2)}) copy-start(bf16[4,256,256]{2,1,0:T(8,128)(2,1)} %param.23) | copy-start | bytes 1572868
  9.9 3.6 %copy-start.2 = (bf16[128,64,256]{2,1,0:T(8,128)(2,1)S(1)}, bf16[128,64,256]{2,1,0:T(8,128)(2,1)}, u32[]{:S(2)}) copy-start(bf16[128,64,256]{2,1,0:T(8,128)(2,1)} %param.17) | copy-start | bytes 12582916
  28.0 7.7 %copy-start.4 = (f32[128,3,3]{0,2,1:T(4,128)S(1)}, f32[128,3,3]{0,2,1:T(4,128)}, u32[]{:S(2)}) copy-start(f32[128,3,3]{0,2,1:T(4,128)} %param.16) | copy-start | bytes 13828
  59.9 8.0 %copy-start.7 = (s32[4]{0:T(128)S(1)}, s32[4]{0:T(128)}, u32[]{:S(2)}) copy-start(s32[4]{0:T(128)} %param.20) | copy-start | bytes 52
  59.9 8.6 %copy-start.3 = (f32[4,3,3]{2,0,1:T(4,128)S(1)}, f32[4,3,3]{2,0,1:T(4,128)}, u32[]{:S(2)}) copy-start(f32[4,3,3]{2,0,1:T(4,128)} %param.22) | copy-start | bytes 436
  62.7 42.5 %all-to-all-start = ((bf16[4,64,6144]{2,1,0:T(8,128)(2,1)}), bf16[4,64,6144]{2,1,0:T(8,128)(2,1)}, u32[]{:S(2)}, u32[]{:S(2)}) async-start(bf16[4,64,6144]{2,1,0:T(8,128)(2,1)} %bitcast.43), calls=%async_computation | async-start | bytes 6291456 | tf_op jit(solution)/shard_map/all_to_all | solution.py:64
  67.9 111.0 %reduce-scatter.3.cloned.1.call-start = ((), (), s32[]{:S(2)}) async-start(), calls=%async_computation.3 | async-start | bytes 983040 | tf_op jit(solution)/shard_map/reduce_scatter | solution.py:91
  114.8 16.9 %copy-start.5 = (s32[256]{0:T(256)S(1)}, s32[256]{0:T(256)}, u32[]{:S(2)}) copy-start(s32[256]{0:T(256)} %param.19) | copy-start | bytes 3076
  131.7 21.2 %copy-start.6 = (s32[4]{0:T(128)S(1)}, s32[4]{0:T(128)}, u32[]{:S(2)}) copy-start(s32[4]{0:T(128)} %param.21) | copy-start | bytes 52
  131.7 56.6 %copy-start.1 = (bf16[4,256,256]{2,1,0:T(8,128)(2,1)S(1)}, bf16[4,256,256]{2,1,0:T(8,128)(2,1)}, u32[]{:S(2)}) copy-start(bf16[4,256,256]{2,1,0:T(8,128)(2,1)} %param.23) | copy-start | bytes 1572868
  155.1 33.2 %reduce-scatter.5.cloned.1.call-start = ((), (), s32[]{:S(2)}) async-start(), calls=%async_computation.4 | async-start | bytes 294912 | tf_op jit(solution)/shard_map/reduce_scatter | solution.py:92
Sparse Core Ops, SparseCore 0:
  155.2 23.6 reduce-scatter.2
  181.1 7.1 reduce-scatter.4
where the time goes:
time: 196 us; the launch traced here: 195 us
  matrix products  73.2 us (37%)
  waiting for transfers between devices  68.6 us (35%)
  local copies, waits for them, and re-layouts  31.2 us (16%)
  between operations  13.6 us (7%)
  starting transfers between devices  5.24 us (3%)
  other arithmetic  3.34 us (2%)
    all_to_all x1, waiting for transfers between devices, body(): lax.all_to_all(outgoing, 'tgt', split_axis=0, concat_axis=0, tiled=True)  35.4 us
    reduce_scatter x1, waiting for transfers between devices, body(): lax.psum_scatter(sectioned, 'src', scatter_dimension=2, tiled=True)  23.8 us
    dot_general x1, matrix products, body(): far_part = jnp.einsum('st,sfq->ftq', far_spread, contrib, precision=highest)  21.2 us
    dot_general x1, matrix products, body(): jnp.einsum('bcd,bdsr->bcsr', mixing, coefficients, precision=highest)  18 us
    dot_general x1, matrix products, body(): jnp.einsum('sfr,srq->sfq', received, u_factor, preferred_element_type=jnp...  16.9 us
    reshape x1, local copies, waits for them, and re-layouts, body(): received = incoming.reshape(slot_count, channels, rank_width)  9.6 us
    reduce_scatter x1, waiting for transfers between devices, body(): lax.psum_scatter(sectioned, 'comp', scatter_dimension=1, tiled=True)  9.36 us
    dot_general x1, matrix products, body(): jnp.einsum('bfp,brp->bfr', selected, v_factor, preferred_element_type=jnp...  9.06 us
  transfers between devices with their start and end apart: 3, of which 3 were waited for; matrix products, arithmetic and copies ran while one was open for 1% of the time, Pallas kernels for 0%

commit v1 on v0

v1 whole, which is shorter than its diff:
```python
import functools

import jax
import jax.numpy as jnp
from jax import lax
from jax.experimental import pallas as pl
from jax.experimental.pallas import tpu as pltpu
from jax.sharding import PartitionSpec as P

NT = (((1,), (1,)), ((), ()))


def mix_rows(weights, value, components):
    rows = value.shape[0] // components
    parts = [value[d * rows : (d + 1) * rows] for d in range(components)]
    mixed = []
    for c in range(components):
        total = weights[c][0] * parts[0]
        for d in range(1, components):
            total = total + weights[c][d] * parts[d]
        mixed.append(total)
    return jnp.concatenate(mixed, axis=0)


def coef_kernel(components, dest, src, ranks, mix, x_ref, v_ref, out_ref, order, count):
    groups, pairs, channels, lanes = out_ref.shape
    width = lanes // 2
    blocks = v_ref.shape[0]
    clusters = x_ref.shape[0] // channels
    capacity = 2 * pairs
    unroll = 4 if pairs % 4 == 0 else 1

    def clear(g, carry):
        count[g] = 0
        return carry

    lax.fori_loop(0, groups, clear, 0)

    def place(b, carry):
        g = dest[b]
        k = count[g]
        order[g * capacity + k] = b
        count[g] = k + 1
        return carry

    lax.fori_loop(0, blocks, place, 0)
    lane = lax.broadcasted_iota(jnp.int32, (1, lanes), 1)
    first = lane < width
    rank_at = lane % width

    def group(g, carry):
        used = count[g]

        def one(m):
            k = 2 * m
            b0 = jnp.where(k < used, order[g * capacity + k], 0)
            b1 = jnp.where(k + 1 < used, order[g * capacity + k + 1], 0)
            r0 = jnp.where(k < used, ranks[b0], 0)
            r1 = jnp.where(k + 1 < used, ranks[b1], 0)
            v = jnp.concatenate([v_ref[b0], v_ref[b1]], axis=0)
            y = lax.dot_general(x_ref[...], v, NT, preferred_element_type=jnp.float32)
            chosen = jnp.where(first, src[b0], src[b1])
            coef = y[:channels]
            for s in range(1, clusters):
                coef = jnp.where(chosen == s, y[s * channels : (s + 1) * channels], coef)
            coef = jnp.where(rank_at < jnp.where(first, r0, r1), coef, 0.0)
            square = components * components
            weights = [
                [
                    jnp.where(
                        first,
                        mix[b0 * square + c * components + d],
                        mix[b1 * square + c * components + d],
                    )
                    for d in range(components)
                ]
                for c in range(components)
            ]
            out_ref[g, m] = mix_rows(weights, coef, components).astype(jnp.bfloat16)

        def several(step, carry):
            for u in range(unroll):
                one(step * unroll + u)
            return carry

        steps = (used + 2 * unroll - 1) // (2 * unroll)
        lax.fori_loop(0, steps, several, 0)

        def blank(m, carry):
            out_ref[g, m] = jnp.zeros((channels, lanes), jnp.bfloat16)
            return carry

        lax.fori_loop(steps * unroll, pairs, blank, 0)
        return carry

    lax.fori_loop(0, groups, group, 0)


def near_kernel(components, near_src, near_tgt, near_mix, x_ref, matrix_ref, out_ref):
    channels = out_ref.shape[1]
    square = components * components
    out_ref[...] = jnp.zeros_like(out_ref)
    for n in range(matrix_ref.shape[0]):
        x = x_ref[pl.ds(pl.multiple_of(near_src[n] * channels, 32), channels), :]
        y = lax.dot_general(x, matrix_ref[n], NT, preferred_element_type=jnp.float32)
        weights = [
            [near_mix[n * square + c * components + d] for d in range(components)]
            for c in range(components)
        ]
        out_ref[near_tgt[n]] += mix_rows(weights, y, components)


def far_kernel(cluster, near_ref, got_ref, u_ref, out_ref):
    step = pl.program_id(0)
    pairs, channels, lanes = got_ref.shape
    first = lax.broadcasted_iota(jnp.int32, (channels, lanes), 1) < lanes // 2
    unroll = 4 if pairs % 4 == 0 else 1

    @pl.when(step == 0)
    def _():
        out_ref[...] = near_ref[...]

    def several(at, carry):
        done = []
        for u in range(unroll):
            m = at * unroll + u
            a = got_ref[m]
            zero = jnp.zeros_like(a)
            both = jnp.concatenate(
                [jnp.where(first, a, zero), jnp.where(first, zero, a)], axis=0
            )
            done.append(
                jnp.dot(both, u_ref[m], preferred_element_type=jnp.float32)
            )
        for u in range(unroll):
            k = 2 * (step * pairs + at * unroll + u)
            out_ref[cluster[k]] += done[u][:channels]
            out_ref[cluster[k + 1]] += done[u][channels:]
        return carry

    lax.fori_loop(0, pairs // unroll, several, 0)


def body(
    field,
    dest_group,
    src_local,
    ranks,
    mixing,
    v_factor,
    u_factor,
    slot_cluster,
    near_src,
    near_tgt,
    near_mixing,
    near_matrix,
):
    groups = lax.axis_size("tgt")
    shards = lax.axis_size("src")
    pairing = lax.axis_size("comp")
    blocks, rank_width, cluster_size = v_factor.shape
    components, vectors, points = field.shape
    channels = components * vectors
    owned = points // cluster_size
    slot_count = u_factor.shape[0]
    capacity = slot_count // groups
    targets = owned * shards
    sources = field.reshape(channels, owned, cluster_size).transpose(1, 0, 2)
    sources = sources.reshape(owned * channels, cluster_size)
    smem = pl.BlockSpec(memory_space=pltpu.SMEM)
    vmem = pl.BlockSpec(memory_space=pltpu.VMEM)
    lanes = 2 * rank_width

    outgoing = pl.pallas_call(
        functools.partial(coef_kernel, components),
        out_shape=jax.ShapeDtypeStruct((groups, capacity // 2, channels, lanes), jnp.bfloat16),
        in_specs=[smem] * 4 + [vmem] * 2,
        out_specs=vmem,
        scratch_shapes=[
            pltpu.SMEM((slot_count,), jnp.int32),
            pltpu.SMEM((groups,), jnp.int32),
        ],
        name="coef",
    )(dest_group.reshape(-1), src_local, ranks, mixing.reshape(-1), sources, v_factor)

    incoming = lax.all_to_all(outgoing, "tgt", split_axis=0, concat_axis=0, tiled=True)

    near_part = pl.pallas_call(
        functools.partial(near_kernel, components),
        out_shape=jax.ShapeDtypeStruct((targets, channels, cluster_size), jnp.float32),
        in_specs=[smem] * 3 + [vmem] * 2,
        out_specs=vmem,
        cost_estimate=pl.CostEstimate(
            flops=2 * near_matrix.size * channels, bytes_accessed=3000000, transcendentals=0
        ),
        name="near",
    )(near_src, near_tgt, near_mixing.reshape(-1), sources, near_matrix)

    pair_count = slot_count // 2
    chunk = 16 if pair_count % 16 == 0 else capacity // 2
    total = pl.pallas_call(
        far_kernel,
        grid=(pair_count // chunk,),
        out_shape=jax.ShapeDtypeStruct((targets, channels, cluster_size), jnp.float32),
        in_specs=[
            smem,
            vmem,
            pl.BlockSpec((chunk, channels, lanes), lambda i: (i, 0, 0)),
            pl.BlockSpec((chunk, lanes, cluster_size), lambda i: (i, 0, 0)),
        ],
        out_specs=vmem,
        compiler_params=pltpu.CompilerParams(dimension_semantics=("arbitrary",)),
        name="far",
    )(
        slot_cluster,
        near_part,
        incoming.reshape(pair_count, channels, lanes),
        u_factor.reshape(pair_count, lanes, cluster_size),
    )

    members = pairing * shards
    kept = targets // members
    pieces = total.reshape(members, kept, channels, cluster_size)
    passed = lax.all_to_all(
        pieces.astype(jnp.bfloat16), ("comp", "src"), split_axis=0, concat_axis=0, tiled=True
    )
    me = lax.axis_index("comp") * shards + lax.axis_index("src")
    own = lax.dynamic_index_in_dim(pieces, me, 0, keepdims=False)
    other = (jnp.arange(members) != me)[:, None, None, None]
    summed = own + jnp.sum(jnp.where(other, passed.astype(jnp.float32), 0.0), axis=0)
    return summed.transpose(1, 0, 2).reshape(components, vectors, kept * cluster_size)


def solution(mesh):
    placed = (
        P(None, None, ("tgt", "src")),
        P(("comp", "tgt", "src"), None),
        P(("comp", "tgt", "src")),
        P(("comp", "tgt", "src")),
        P(("comp", "tgt", "src"), None, None),
        P(("comp", "tgt", "src"), None, None),
        P(("comp", "tgt", "src"), None, None),
        P(("comp", "tgt", "src")),
        P(("comp", "tgt", "src")),
        P(("comp", "tgt", "src")),
        P(("comp", "tgt", "src"), None, None),
        P(("comp", "tgt", "src"), None, None),
    )
    return jax.shard_map(
        body,
        mesh=mesh,
        in_specs=placed,
        out_specs=P(None, None, ("comp", "tgt", "src")),
        check_vma=False,
    )
```

time: 196 us -> 91 us (0.46)
  matrix products: 73.2 us -> 0 us
  local copies, waits for them, and re-layouts: 31.2 us -> 5.49 us
  Pallas kernels: 0 us -> 25.7 us
  waiting for transfers between devices: 68.6 us -> 45.4 us
  between operations: 13.6 us -> 0.02 us
  starting transfers between devices: 5.24 us -> 10.2 us
    dot_general x10 -> x0, matrix products: 73.2 us -> none  [the longest x1 21.2 us: body(): far_part = jnp.einsum('st,sfq->ftq', far_spread, contrib, precision=highest)]
    reduce_scatter x2 -> x0, waiting for transfers between devices: 33.1 us -> none  [the longest x1 23.8 us: body(): lax.psum_scatter(sectioned, 'src', scatter_dimension=2, tiled=True)]
    pallas_call x0 -> x3, Pallas kernels: none -> 25.7 us  [the longest x1 12.2 us: body(): pl.pallas_call(far_kernel, grid=(pair_count // chunk,), out_shape=jax.Sha...]
    reshape x5 -> x4, local copies, waits for them, and re-layouts: 19.6 us -> 2.98 us  [the longest x2 1.57 us: body(): sources = field.reshape(channels, owned, cluster_size).transpose(1, 0, 2)]
    all_to_all x0 -> x1, waiting for transfers between devices: none -> 12 us  [body(): lax.all_to_all(pieces.astype(jnp.bfloat16), ('comp', 'src'), split_axis=0...]
    convert_element_type x1 -> x0, local copies, waits for them, and re-layouts: 5.95 us -> none  [body(): mixed_coef.reshape(blocks, channels * rank_width).astype(jnp.bfloat16)]
    mul x1 -> x0, local copies, waits for them, and re-layouts: 5.36 us -> none  [body(): coefficients * rank_mask[:, None, :]]
    all_to_all x0 -> x1, starting transfers between devices: none -> 5.13 us  [body(): lax.all_to_all(pieces.astype(jnp.bfloat16), ('comp', 'src'), split_axis=0...]
  transfers between devices with their start and end apart: 3 -> 2, of which waited for: 3 -> 2; matrix products, arithmetic and copies ran while one was open for 1% -> 1% of each run, Pallas kernels for 0% -> 3%
where the time goes in v1:
time: 91 us; the launch traced here: 90.5 us
  waiting for transfers between devices  45.4 us (50%)
  Pallas kernels  25.7 us (28%)
  starting transfers between devices  10.2 us (11%)
  local copies, waits for them, and re-layouts  5.49 us (6%)
  other arithmetic  3.63 us (4%)
    all_to_all x1, waiting for transfers between devices, body(): lax.all_to_all(outgoing, 'tgt', split_axis=0, concat_axis=0, tiled=True)  33.4 us
    pallas_call x1, Pallas kernels, body(): pl.pallas_call(far_kernel, grid=(pair_count // chunk,), out_shape=jax.Sha...  12.2 us
    all_to_all x1, waiting for transfers between devices, body(): lax.all_to_all(pieces.astype(jnp.bfloat16), ('comp', 'src'), split_axis=0...  12 us
    pallas_call x1, Pallas kernels, body(): pl.pallas_call(functools.partial(coef_kernel, components), out_shape=jax....  11.2 us
    all_to_all x1, starting transfers between devices, body(): lax.all_to_all(pieces.astype(jnp.bfloat16), ('comp', 'src'), split_axis=0...  5.13 us
    all_to_all x1, starting transfers between devices, body(): lax.all_to_all(outgoing, 'tgt', split_axis=0, concat_axis=0, tiled=True)  5.09 us
    unnamed x6, local copies, waits for them, and re-layouts  2.51 us
    pallas_call x1, Pallas kernels, body(): pl.pallas_call(functools.partial(near_kernel, components), out_shape=jax....  2.31 us
  transfers between devices with their start and end apart: 2, of which 2 were waited for; matrix products, arithmetic and copies ran while one was open for 1% of the time, Pallas kernels for 3%

profile of v1, /device:TPU:0, one launch (start us, length us, event | category | flops | bytes accessed | tf_op | source)
XLA Modules:
  0.0 90.5 jit_solution(229069009661202866)
XLA Ops:
  0.0 0.9 %reshape.36 = bf16[96,2,256]{2,1,0:T(2,128)(2,1)S(1)} reshape(bf16[3,32,512]{2,1,0:T(8,128)(2,1)} %param.12) | data formatting | bytes 196608 | tf_op jit(solution)/shard_map/reshape | solution.py:168
  0.9 0.7 copy.19
  1.6 0.9 copy.20
  2.4 0.8 reshape.39.mix
  3.2 11.2 %coef.1 = bf16[4,32,96,128]{3,2,1,0:T(8,128)(2,1)} custom-call(s32[128]{0:T(128)} %bitcast.17, s32[128]{0:T(128)} %src.1, s32[128]{0:T(128)} %ranks.1, f32[1152]{0:T(1024)} %reshape.39.mix, bf16[192,256]{1,0:T(8,128)(2,1)} %bitcast.15, bf16[128,64,256]{2,1,0:T(8,128)(2,1)} %v_ref.1), custom_call_target="tpu_custom_call" | custom-call | tf_op jit(solution)/shard_map/coef/pallas_call | solution.py:174
  14.5 0.0 copy-start.1
  14.5 5.1 %all-to-all-start = ((bf16[4,32,96,128]{3,2,1,0:T(8,128)(2,1)}), bf16[4,32,96,128]{3,2,1,0:T(8,128)(2,1)S(1)}, u32[]{:S(2)}, u32[]{:S(2)}) async-start(bf16[4,32,96,128]{3,2,1,0:T(8,128)(2,1)} %coef.1), calls=%async_computation | async-start | bytes 6291456 | tf_op jit(solution)/shard_map/all_to_all | solution.py:186
  19.6 0.0 copy-done.1
  19.6 0.6 reshape.35.near_mix
  20.2 2.3 %near.1.near_ref = f32[8,96,256]{2,1,0:T(8,128)} custom-call(s32[4]{0:T(128)} %near_src.1, s32[4]{0:T(128)} %near_tgt.1, f32[36]{0:T(128)} %reshape.35.near_mix, bf16[192,256]{1,0:T(8,128)(2,1)} %bitcast.16, bf16[4,256,256]{2,1,0:T(8,128)(2,1)} %matrix_ref.1), custom_call_target="tpu_custom_call" | custom-call | flops 50331648 | bytes 3000000 | tf_op jit(solution)/shard_map/near/pallas_call | solution.py:188
  22.5 33.4 %all-to-all-done = bf16[4,32,96,128]{3,2,1,0:T(8,128)(2,1)S(1)} async-done(((bf16[4,32,96,128]{3,2,1,0:T(8,128)(2,1)}), bf16[4,32,96,128]{3,2,1,0:T(8,128)(2,1)S(1)}, u32[]{:S(2)}, u32[]{:S(2)}) %all-to-all-start) | async-done | bytes 3145760 | tf_op jit(solution)/shard_map/all_to_all | solution.py:186
  55.9 0.0 copy-start
  55.9 1.6 %copy-done = bf16[4,32,96,128]{3,2,1,0:T(8,128)(2,1)} copy-done((bf16[4,32,96,128]{3,2,1,0:T(8,128)(2,1)}, bf16[4,32,96,128]{3,2,1,0:T(8,128)(2,1)S(1)}, u32[]{:S(2)}) %copy-start) | copy-done | bytes 3145752
  57.5 12.2 %far.1 = f32[8,96,256]{2,1,0:T(8,128)} custom-call(s32[256]{0:T(256)} %cluster.1, f32[8,96,256]{2,1,0:T(8,128)} %near.1.near_ref, bf16[128,96,128]{2,1,0:T(8,128)(2,1)} %bitcast.13, bf16[128,128,256]{2,1,0:T(8,128)(2,1)} %bitcast.14), custom_call_target="tpu_custom_call" | custom-call | tf_op jit(solution)/shard_map/far/pallas_call | solution.py:201
  69.7 1.9 %convert_bitcast_fusion = bf16[8,1,96,256]{3,2,1,0:T(8,128)(2,1)} fusion(f32[8,96,256]{2,1,0:T(8,128)} %far.1), kind=kLoop, calls=%fused_computation.1 | loop fusion | flops 196608 | bytes 1179648 | tf_op jit(solution)/shard_map/convert_element_type | solution.py:225
  71.7 5.1 %all-to-all-start.1 = ((bf16[8,1,96,256]{3,2,1,0:T(8,128)(2,1)}), bf16[8,1,96,256]{3,2,1,0:T(8,128)(2,1)S(1)}, u32[]{:S(2)}, u32[]{:S(2)}) async-start(bf16[8,1,96,256]{3,2,1,0:T(8,128)(2,1)} %convert_bitcast_fusion), calls=%async_computation.1 | async-start | bytes 786432 | tf_op jit(solution)/shard_map/all_to_all | solution.py:224
  76.8 12.0 %all-to-all-done.1 = bf16[8,1,96,256]{3,2,1,0:T(8,128)(2,1)S(1)} async-done(((bf16[8,1,96,256]{3,2,1,0:T(8,128)(2,1)}), bf16[8,1,96,256]{3,2,1,0:T(8,128)(2,1)S(1)}, u32[]{:S(2)}, u32[]{:S(2)}) %all-to-all-start.1) | async-done | bytes 393248 | tf_op jit(solution)/shard_map/all_to_all | solution.py:224
  88.8 0.1 select_reduce_fusion
  88.9 1.6 %bitcast_add_fusion = f32[1,96,256]{2,1,0:T(8,128)} fusion(f32[96,256]{1,0:T(8,128)S(1)} %select_reduce_fusion, f32[8,96,256]{2,1,0:T(8,128)} %far.1, s32[]{:T(128)S(6)} %select_n.8), kind=kLoop, calls=%fused_computation.2 | loop fusion | flops 24576 | bytes 294916 | tf_op jit(solution)/shard_map/add | solution.py:230
  (2 shorter events, 0.0 us)
Async XLA Ops:
  14.5 5.1 %copy-start.1 = (f32[4,3,3]{2,0,1:T(4,128)S(1)}, f32[4,3,3]{2,0,1:T(4,128)}, u32[]{:S(2)}) copy-start(f32[4,3,3]{2,0,1:T(4,128)} %param.22) | copy-start | bytes 436
  14.5 41.4 %all-to-all-start = ((bf16[4,32,96,128]{3,2,1,0:T(8,128)(2,1)}), bf16[4,32,96,128]{3,2,1,0:T(8,128)(2,1)S(1)}, u32[]{:S(2)}, u32[]{:S(2)}) async-start(bf16[4,32,96,128]{3,2,1,0:T(8,128)(2,1)} %coef.1), calls=%async_computation | async-start | bytes 6291456 | tf_op jit(solution)/shard_map/all_to_all | solution.py:186
  55.9 1.6 %copy-start = (bf16[4,32,96,128]{3,2,1,0:T(8,128)(2,1)}, bf16[4,32,96,128]{3,2,1,0:T(8,128)(2,1)S(1)}, u32[]{:S(2)}) copy-start(bf16[4,32,96,128]{3,2,1,0:T(8,128)(2,1)S(1)} %all-to-all-done) | copy-start | bytes 9437188
  71.7 17.1 %all-to-all-start.1 = ((bf16[8,1,96,256]{3,2,1,0:T(8,128)(2,1)}), bf16[8,1,96,256]{3,2,1,0:T(8,128)(2,1)S(1)}, u32[]{:S(2)}, u32[]{:S(2)}) async-start(bf16[8,1,96,256]{3,2,1,0:T(8,128)(2,1)} %convert_bitcast_fusion), calls=%async_computation.1 | async-start | bytes 786432 | tf_op jit(solution)/shard_map/all_to_all | solution.py:224
